TPU v7x, 32 devices: a whole 2x2x4 slice. The times are simulated.
32 devices in a mesh: dp: 4 (over x, core), row: 2 (over y), col: 4 (over z).
Axes of the slice: x: 2, y: 2, z: 4, core: 2. Of those that a mesh axis runs over, the one named last changes fastest.
Arguments:
- act_in: bfloat16 [4096, 2304], P(('dp', 'row'), 'col'), may hold values from -6 to 6
- cot_out: bfloat16 [4096, 2304], P(('dp', 'row'), 'col'), may hold values from -6 to 6
- w_gate: bfloat16 [2304, 4608], P(('dp', 'row'), 'col'), may hold values from -0.125 to 0.125
- w_up: bfloat16 [2304, 4608], P(('dp', 'row'), 'col'), may hold values from -0.125 to 0.125
- w_down: bfloat16 [4608, 2304], P('col', ('dp', 'row')), may hold values from -0.09375 to 0.09375
Outputs:
- input_grad: bfloat16 [4096, 2304], P(('dp', 'row'), 'col')
- gate_grad: float32 [2304, 4608], P(('dp', 'row'), 'col')
- up_grad: float32 [2304, 4608], P(('dp', 'row'), 'col')
- down_grad: float32 [4608, 2304], P('col', ('dp', 'row'))
All inputs are finite; a program needn't handle non-finite values.
Results may differ from a plain program's by a relative error of at most 0.015.
Values may be sent and summed in bfloat16 or wider, within the bound.
A program may use at most 128 MiB of HBM per device.

v0:
```python
import functools
import math

import jax
import jax.numpy as jnp
from jax import lax
from jax.experimental import pallas as pl
from jax.experimental.pallas import tpu as pltpu
from jax.sharding import PartitionSpec as P

gelu_cubic = 0.044715
gelu_scale = 0.7978845608028654
MESH = pl.DeviceIdType.MESH
F32 = jnp.float32
BF16 = jnp.bfloat16


def gelu_parts(values):
    inner_arg = gelu_scale * (values + gelu_cubic * values * values * values)
    tanh_val = jnp.tanh(inner_arg)
    output = 0.5 * values * (1.0 + tanh_val)
    slope_val = 0.5 * (1.0 + tanh_val) + 0.5 * values * (1.0 - tanh_val * tanh_val) * gelu_scale * (
        1.0 + 3.0 * gelu_cubic * values * values
    )
    return (output, slope_val)


def tile_of(size, best):
    return best if size % best == 0 else size


def pieces_of(rows):
    if rows % 32 == 0:
        return [(0, 0, rows, 0), (1, 0, rows, 1), (2, 0, rows // 2, 0), (2, rows // 2, rows // 2, 1)]
    return [(0, 0, rows, 0), (1, 0, rows, 1), (2, 0, rows, 0)]


def others_first(n):
    return list(range(1, n)) + [0]


class Sends:
    def __init__(self, sems):
        self.sems, self.used, self.pending = sems, 0, []

    def start(self, src, dst, recv_sem, where, cond=None):
        copy = pltpu.make_async_remote_copy(
            src_ref=src,
            dst_ref=dst,
            send_sem=self.sems.at[self.used],
            recv_sem=recv_sem,
            device_id=where,
            device_id_type=MESH,
        )
        self.used += 1
        self.pending.append((cond, copy))
        guarded(cond, copy.start)

    def finish(self):
        for cond, copy in self.pending:
            guarded(cond, copy.wait_send)


def guarded(cond, action):
    if cond is None:
        action()
    else:
        pl.when(cond)(action)


def arrived(ref, sem):
    pltpu.make_async_copy(ref, ref, sem).wait()


def kernel(sizes, act_ref, cot_ref, wg_ref, wu_ref, wd_ref, ig_ref, og_ref, ou_ref, od_ref,
           full, weights, grads, stash, partner_out, sums, first_in, second_in, ig_out, ig_in,
           own_sem, send_sem, w_sem, x_sem, pair_send, pair_recv, first_sem, second_sem, ig_sem):
    n_dp, n_row, n_col, rows, hid, feats, toks = sizes
    nq, ny = n_dp // 2, n_row
    peers = nq * ny
    pieces = pieces_of(rows)
    dp, y, col = lax.axis_index("dp"), lax.axis_index("row"), lax.axis_index("col")
    q, c = dp // 2, dp % 2
    rep_of = lambda q1, c1, y1: (q1 * 2 + c1) * ny + y1
    at_q = lambda dq: lax.rem(q + dq, nq)
    at_y = lambda dy: lax.rem(y + dy, ny)
    back_q = lambda dq: lax.rem(q + nq - dq, nq)
    back_y = lambda dy: lax.rem(y + ny - dy, ny)
    me = rep_of(q, c, y)
    partner = {"dp": q * 2 + 1 - c}
    q_peer = lambda dq: {"dp": at_q(dq) * 2 + c}
    y_peer = lambda dy: {"row": at_y(dy)}

    barrier = pltpu.get_barrier_semaphore()
    friends = [partner] + [q_peer(i) for i in range(1, nq)] + [y_peer(i) for i in range(1, ny)]
    friends += [{"col": lax.rem(col + i, n_col)} for i in range(1, n_col)]
    for friend in friends:
        pl.semaphore_signal(barrier, inc=1, device_id=friend, device_id_type=MESH)
    pl.semaphore_wait(barrier, len(friends))

    sends = Sends(send_sem)
    mine = (wg_ref, wu_ref, wd_ref)
    streams = (act_ref, cot_ref)

    def rows_at(rep, r0, nr):
        return pl.ds(pl.multiple_of(rep * rows + r0, 8), nr)

    def slot(p, rep):
        w, r0, nr, _ = pieces[p]
        return weights.at[w, rows_at(rep, r0, nr), :]

    half = feats // 2

    def feat_slot(s, h, block):
        return full.at[s, pl.ds(pl.multiple_of(block * feats + h * half, 8), half), :]

    def feat_sem(s, h, block):
        return x_sem.at[(s * 2 + h) * n_col + block]

    has_right, has_left = col < n_col - 1, col > 0
    right = {"col": jnp.minimum(col + 1, n_col - 1)}
    left = {"col": jnp.maximum(col - 1, 0)}

    def own_features(s):
        for h in range(2):
            src = streams[s].at[pl.ds(h * half, half), :]
            sends.start(src, feat_slot(s, h, col), feat_sem(s, h, col), right, has_right)
            sends.start(src, feat_slot(s, h, col), feat_sem(s, h, col), left, has_left)

    def own_weight(weight):
        for p, (w, r0, nr, route) in enumerate(pieces):
            if w != weight:
                continue
            src = mine[w].at[pl.ds(r0, nr), :]
            sem = w_sem.at[p * peers * 2 + me]
            for dq in range(1, nq):
                sends.start(src, slot(p, me), sem, q_peer(dq))
            for dy in range(1, ny):
                sends.start(src, slot(p, me), sem, y_peer(dy))
            sends.start(src, slot(p, me), sem, partner)

    own_features(0)
    own_weight(0)
    own_weight(1)
    locals_ = []
    for i, (src, dst) in enumerate(
        [(streams[s], full.at[s, pl.ds(pl.multiple_of(col * feats, 8), feats), :]) for s in range(2)]
        + [(mine[w], weights.at[w, rows_at(me, 0, rows), :]) for w in range(3)]
    ):
        locals_.append(pltpu.make_async_copy(src, dst, own_sem.at[i]))
        locals_[-1].start()

    def chain(s, step):
        from_left, from_right = col >= step, col + step < n_col
        lb, rb = jnp.maximum(col - step, 0), jnp.minimum(col + step, n_col - 1)
        for h in range(2):
            l_slot, l_sem = feat_slot(s, h, lb), feat_sem(s, h, lb)
            r_slot, r_sem = feat_slot(s, h, rb), feat_sem(s, h, rb)
            guarded(from_left, lambda: arrived(l_slot, l_sem))
            if step < n_col - 1:
                sends.start(l_slot, l_slot, l_sem, right, from_left & has_right)
            guarded(from_right, lambda: arrived(r_slot, r_sem))
            if step < n_col - 1:
                sends.start(r_slot, r_slot, r_sem, left, from_right & has_left)

    def take(p, rep, forward):
        sem = w_sem.at[p * peers * 2 + rep]
        arrived(slot(p, rep), sem)
        for where in forward + [partner]:
            sends.start(slot(p, rep), slot(p, rep), sem, where)

    def near(p):
        route = pieces[p][3]
        for dq in range(1, nq):
            take(p, rep_of(back_q(dq), c, y), [y_peer(i) for i in range(1, ny)] if route == 0 else [])
        for dy in range(1, ny):
            take(p, rep_of(q, c, back_y(dy)), [q_peer(i) for i in range(1, nq)] if route == 1 else [])

    def far(p):
        for dq in range(1, nq):
            for dy in range(1, ny):
                take(p, rep_of(back_q(dq), c, back_y(dy)), [])

    def from_partner(p):
        for dq in range(nq):
            for dy in range(ny):
                rep = rep_of(at_q(dq), 1 - c, at_y(dy))
                arrived(slot(p, rep), w_sem.at[p * peers * 2 + rep])

    near(0)
    chain(0, 1)
    near(1)
    own_weight(2)
    for step in range(2, n_col):
        if step == n_col - 1:
            own_features(1)
        chain(0, step)
    far(0)
    far(1)
    from_partner(0)
    from_partner(1)
    for copy in locals_:
        copy.wait()

    mt, nt = tile_of(toks, 256), tile_of(hid, 384)
    m_tiles, n_tiles = toks // mt, hid // nt
    token_dims = (((0,), (0,)), ((), ()))
    later = [p for p in range(len(pieces)) if pieces[p][0] == 2]

    def tile_slices(i):
        m, n = i // n_tiles, i % n_tiles
        return pl.ds(pl.multiple_of(m * mt, mt), mt), pl.ds(pl.multiple_of(n * nt, nt), nt)

    def project(first, last):
        @pl.loop(first, last)
        def _(i):
            ms, ns = tile_slices(i)
            x = full[0, :, ms]
            gate_pre = lax.dot_general(x, weights[0, :, ns], token_dims, preferred_element_type=F32)
            up_pre = lax.dot_general(x, weights[1, :, ns], token_dims, preferred_element_type=F32)
            act_val, slope_val = gelu_parts(gate_pre)
            grads[2, ms, ns] = (act_val * up_pre).astype(BF16)
            stash[0, ms, ns] = up_pre * slope_val
            stash[1, ms, ns] = act_val

    tiles = m_tiles * n_tiles
    project(0, tiles // 2)
    chain(1, 1)
    project(tiles // 2, tiles)
    for p in later:
        near(p)
    for step in range(2, n_col - 1):
        chain(1, step)

    def term(w, rep, ns):
        return jnp.dot(full[w // 2, rows_at(rep, 0, rows), :], grads[w, :, ns], preferred_element_type=F32)

    def n_slice(n):
        return pl.ds(pl.multiple_of(n * nt, nt), nt)

    def pair_copy(i):
        return pltpu.make_async_remote_copy(
            src_ref=partner_out.at[i],
            dst_ref=sums.at[i],
            send_sem=pair_send.at[i],
            recv_sem=pair_recv.at[i],
            device_id=partner,
            device_id_type=MESH,
        )

    def is_far(rep):
        block = (rep * rows) // feats
        return jnp.abs(block - col) == n_col - 1

    def partner_terms(w, when=None):
        @pl.loop(0, peers)
        def _(peer):
            i = w * peers + peer
            rep = rep_of(peer // ny, 1 - c, peer % ny)

            def one():
                @pl.loop(0, n_tiles)
                def _(n):
                    partner_out[i, :, n_slice(n)] = term(w, rep, n_slice(n)).astype(BF16)

                pair_copy(i).start()

            guarded(None if when is None else when(rep), one)

    first_base, count = [], 0
    for _, _, _, route in pieces:
        first_base.append(count)
        count += (nq - 1) * ny if route == 0 else (ny - 1) * nq
    second_base, count = [], 0
    for _, _, _, route in pieces:
        second_base.append(count)
        count += (ny - 1) if route == 0 else (nq - 1)

    def first_slot(p, dq, dy):
        k = first_base[p] + ((dq - 1) * ny + dy if pieces[p][3] == 0 else (dy - 1) * nq + dq)
        return first_in.at[k, pl.ds(0, pieces[p][2]), :], first_sem.at[k]

    def second_slot(p, d):
        k = second_base[p] + d - 1
        return second_in.at[k, pl.ds(0, pieces[p][2]), :], second_sem.at[k]

    def own_terms(w, when=None):
        for dq in others_first(nq):
            for dy in others_first(ny):
                index = w * peers + at_q(dq) * ny + at_y(dy)
                rep = rep_of(at_q(dq), c, at_y(dy))
                cond = None if when is None else when(rep)

                def one():
                    arrived(sums.at[index], pair_recv.at[index])

                    @pl.loop(0, n_tiles)
                    def _(n):
                        ns = n_slice(n)
                        sums[index, :, ns] = (term(w, rep, ns) + sums[index, :, ns].astype(F32)).astype(BF16)

                guarded(cond, one)
                for p, (pw, r0, nr, route) in enumerate(pieces):
                    if pw == w and (dq if route == 0 else dy):
                        dst, sem = first_slot(p, dq, dy)
                        where = q_peer(dq) if route == 0 else y_peer(dy)
                        sends.start(sums.at[index, pl.ds(r0, nr), :], dst, sem, where, cond)

    rt = tile_of(feats, 288)
    hid_dims = (((1,), (1,)), ((), ()))

    def input_part(dz):
        block = lax.rem(col + dz, n_col)

        @pl.loop(0, feats // rt)
        def _(r):
            rs = pl.ds(pl.multiple_of(block * feats + r * rt, 8), rt)
            part = lax.dot_general(weights[0, rs, :], grads[0], hid_dims, preferred_element_type=F32)
            part = part + lax.dot_general(weights[1, rs, :], grads[1], hid_dims, preferred_element_type=F32)
            ig_out[dz, pl.ds(pl.multiple_of(r * rt, 8), rt), :] = part.astype(BF16)

        if dz:
            sends.start(ig_out.at[dz], ig_in.at[dz - 1], ig_sem.at[dz - 1], {"col": block})

    outs = (og_ref, ou_ref, od_ref)

    def second(p):
        w, r0, nr, route = pieces[p]
        rs = pl.ds(r0, nr)
        n_first, n_second = (nq, ny) if route == 0 else (ny, nq)
        for d in others_first(n_second):
            index = w * peers + (q * ny + at_y(d) if route == 0 else at_q(d) * ny + y)
            total = sums[index, rs, :].astype(F32)
            for f in range(1, n_first):
                ref, sem = first_slot(p, f, d) if route == 0 else first_slot(p, d, f)
                arrived(ref, sem)
                total = total + ref[...].astype(F32)
            if d:
                sums[index, rs, :] = total.astype(BF16)
                dst, sem = second_slot(p, d)
                sends.start(sums.at[index, rs, :], dst, sem, y_peer(d) if route == 0 else q_peer(d))
            else:
                outs[w][rs, :] = total

    near_rep = lambda rep: jnp.logical_not(is_far(rep))
    partner_terms(2, near_rep)
    own_terms(2, near_rep)
    for p in later:
        far(p)
    for p in later:
        from_partner(p)
    chain(1, n_col - 1)
    partner_terms(2, is_far)

    @pl.loop(0, tiles)
    def _(i):
        ms, ns = tile_slices(i)
        hidden_grad = lax.dot_general(full[1, :, ms], weights[2, :, ns], token_dims, preferred_element_type=F32)
        grads[0, ms, ns] = (hidden_grad * stash[0, ms, ns]).astype(BF16)
        grads[1, ms, ns] = (hidden_grad * stash[1, ms, ns]).astype(BF16)

    own_terms(2, is_far)
    spare = list(range(1, n_col))
    partner_terms(0)
    partner_terms(1)
    input_part(spare.pop(0))
    own_terms(0)
    own_terms(1)
    while spare:
        input_part(spare.pop(0))
    for p in later:
        second(p)
    input_part(0)
    for p in range(len(pieces)):
        if p not in later:
            second(p)

    total = ig_out[0].astype(F32)
    for dz in range(1, n_col):
        arrived(ig_in.at[dz - 1], ig_sem.at[dz - 1])
        total = total + ig_in[dz - 1].astype(F32)
    ig_ref[...] = total.astype(BF16)

    for p, (w, r0, nr, route) in enumerate(pieces):
        rs = pl.ds(r0, nr)
        for d in range(1, ny if route == 0 else nq):
            ref, sem = second_slot(p, d)
            arrived(ref, sem)
            outs[w][rs, :] = outs[w][rs, :] + ref[...].astype(F32)

    sends.finish()

    @pl.loop(0, 3 * peers)
    def _(i):
        pair_copy(i).wait_send()


def body(n_dp, n_row, n_col, act_in, cot_out, w_gate, w_up, w_down):
    toks, feats = act_in.shape
    rows, hid = w_gate.shape
    sizes = (n_dp, n_row, n_col, rows, hid, feats, toks)
    nq, ny = n_dp // 2, n_row
    peers, reps, dim = nq * ny, n_dp * n_row, feats * n_col
    pieces = pieces_of(rows)
    firsts = sum((nq - 1) * ny if r == 0 else (ny - 1) * nq for _, _, _, r in pieces)
    seconds = sum((ny - 1) if r == 0 else (nq - 1) for _, _, _, r in pieces)
    near_far = sum((nq - 1) * (ny - 1) for _ in pieces)
    n_sends = 8 + 8 * (n_col - 2) + len(pieces) * (nq + ny - 1) + len(pieces) * (peers - 1) + near_far
    n_sends += 2 * firsts + seconds + n_col - 1
    any_spec, vmem_spec = pl.BlockSpec(memory_space=pl.ANY), pl.BlockSpec(memory_space=pltpu.VMEM)
    dma = lambda n: pltpu.SemaphoreType.DMA((max(n, 1),))
    wgrad = jax.ShapeDtypeStruct((rows, hid), F32)
    ig_t, gate_grad, up_grad, down_t = pl.pallas_call(
        functools.partial(kernel, sizes),
        out_shape=[jax.ShapeDtypeStruct((feats, toks), BF16), wgrad, wgrad, wgrad],
        in_specs=[any_spec] * 5,
        out_specs=[vmem_spec] * 4,
        scratch_shapes=[
            pltpu.VMEM((2, dim, toks), BF16),
            pltpu.VMEM((3, dim, hid), BF16),
            pltpu.VMEM((3, toks, hid), BF16),
            pltpu.VMEM((2, toks, hid), F32),
            pltpu.VMEM((3 * peers, rows, hid), BF16),
            pltpu.VMEM((3 * peers, rows, hid), BF16),
            pltpu.VMEM((max(firsts, 1), rows, hid), BF16),
            pltpu.VMEM((max(seconds, 1), rows, hid), BF16),
            pltpu.VMEM((n_col, feats, toks), BF16),
            pltpu.VMEM((max(n_col - 1, 1), feats, toks), BF16),
            dma(5), dma(n_sends), dma(len(pieces) * reps), dma(4 * n_col), dma(3 * peers), dma(3 * peers),
            dma(firsts), dma(seconds), dma(n_col - 1),
        ],
        compiler_params=pltpu.CompilerParams(
            collective_id=0, has_side_effects=True, vmem_limit_bytes=67043328
        ),
    )(act_in.T, cot_out.T, w_gate, w_up, w_down.T)
    norm_scale = 1.0 / math.sqrt(toks * n_dp * n_row)
    return (ig_t.T, gate_grad * norm_scale, up_grad * norm_scale, (down_t * norm_scale).T)


def solution(mesh):
    grid = P(("dp", "row"), "col")
    flipped = P("col", ("dp", "row"))
    return jax.shard_map(
        functools.partial(body, mesh.shape["dp"], mesh.shape["row"], mesh.shape["col"]),
        mesh=mesh,
        in_specs=(grid, grid, grid, grid, flipped),
        out_specs=(grid, grid, grid, flipped),
        check_vma=False,
    )
```

profile of v0, /device:TPU:5, one launch (start us, length us, event | category | flops | bytes accessed | tf_op | source)
XLA Modules:
  0.0 168.1 jit_solution(2866985986361325766)
XLA Ops:
  0.6 162.3 %shard_map.84 = (bf16[576,512]{1,0:T(8,128)(2,1)}, f32[288,1152]{1,0:T(8,128)}, f32[288,1152]{1,0:T(8,128)}, f32[288,1152]{1,0:T(8,128)}) custom-call(bf16[576,512]{1,0:T(8,128)(2,1)} %bitcast.8, bf16[576,512]{1,0:T(8,128)(2,1)} %bitcast.9, bf16[288,1152]{1,0:T(8,128)(2,1)} %wg_ref.1, bf16[288,1152]{1,0:T(8,128)(2,1)} %wu_ref.1, bf16[288,1152]{1,0:T(8,128)(2,1)} %bitcast.6), custom_call_target="tpu_custom_call" | custom-call | tf_op jit(solution)/shard_map/pallas_call | solution.py:413
  162.9 0.0 copy-start
  162.9 0.0 copy-start.1
  162.9 2.6 %broadcast_multiply_fusion.1 = f32[288,1152]{1,0:T(8,128)} fusion(f32[288,1152]{1,0:T(8,128)} %get-tuple-element.9), kind=kLoop, calls=%fused_computation.2 | loop fusion | flops 331776 | bytes 2654208 | tf_op jit(solution)/shard_map/mul | solution.py:437
  165.6 0.0 copy-done
  165.6 0.0 copy-done.1
  165.6 0.0 copy-start.2
  165.6 1.7 multiply_bitcast_fusion
  167.2 0.0 copy-done.2
  167.2 0.8 copy.10
Async XLA Ops:
  162.9 2.6 %copy-start = (f32[288,1152]{1,0:T(8,128)S(1)}, f32[288,1152]{1,0:T(8,128)}, u32[]{:S(2)}) copy-start(f32[288,1152]{1,0:T(8,128)} %get-tuple-element.10) | copy-start | bytes 3981316
  162.9 2.6 %copy-start.1 = (f32[288,1152]{1,0:T(8,128)S(1)}, f32[288,1152]{1,0:T(8,128)}, u32[]{:S(2)}) copy-start(f32[288,1152]{1,0:T(8,128)} %get-tuple-element.11) | copy-start | bytes 3981316
  165.6 1.7 copy-start.2
where the time goes:
time: 170 us; the launch traced here: 168 us
  Pallas kernels  162 us (95%)
  other arithmetic  4.29 us (3%)
    pallas_call x1, Pallas kernels, body(): pl.pallas_call(functools.partial(kernel, sizes), out_shape=[jax.ShapeDtyp...  162 us

commit v1 on v0

v1 whole, which is shorter than its diff:
```python
import functools
import math

import jax
import jax.numpy as jnp
from jax import lax
from jax.experimental import pallas as pl
from jax.experimental.pallas import tpu as pltpu
from jax.sharding import PartitionSpec as P

gelu_cubic = 0.044715
gelu_scale = 0.7978845608028654
MESH = pl.DeviceIdType.MESH
F32 = jnp.float32
BF16 = jnp.bfloat16


def gelu_parts(values):
    inner_arg = gelu_scale * (values + gelu_cubic * values * values * values)
    tanh_val = jnp.tanh(inner_arg)
    output = 0.5 * values * (1.0 + tanh_val)
    slope_val = 0.5 * (1.0 + tanh_val) + 0.5 * values * (1.0 - tanh_val * tanh_val) * gelu_scale * (
        1.0 + 3.0 * gelu_cubic * values * values
    )
    return (output, slope_val)


def tile_of(size, best):
    return best if size % best == 0 else size


def pieces_of(rows):
    if rows % 32 == 0:
        return [(0, 0, rows, 0), (1, 0, rows, 1), (2, 0, rows // 2, 0), (2, rows // 2, rows // 2, 1)]
    return [(0, 0, rows, 0), (1, 0, rows, 1), (2, 0, rows, 0)]


def others_first(n):
    return list(range(1, n)) + [0]


class Sends:
    def __init__(self, sems):
        self.sems, self.used, self.pending = sems, 0, []

    def start(self, src, dst, recv_sem, where, cond=None):
        copy = pltpu.make_async_remote_copy(
            src_ref=src,
            dst_ref=dst,
            send_sem=self.sems.at[self.used],
            recv_sem=recv_sem,
            device_id=where,
            device_id_type=MESH,
        )
        self.used += 1
        self.pending.append((cond, copy))
        guarded(cond, copy.start)

    def finish(self):
        for cond, copy in self.pending:
            guarded(cond, copy.wait_send)


def guarded(cond, action):
    if cond is None:
        action()
    else:
        pl.when(cond)(action)


def arrived(ref, sem):
    pltpu.make_async_copy(ref, ref, sem).wait()


def kernel(sizes, act_ref, cot_ref, wg_ref, wu_ref, wd_ref, ig_ref, og_ref, ou_ref, od_ref,
           full, weights, grads, stash, acc, partner_out, sums, first_in, second_in, ig_out, ig_in, outs,
           own_sem, send_sem, w_sem, x_sem, pair_send, pair_recv, first_sem, second_sem, ig_sem, out_sem):
    n_dp, n_row, n_col, rows, hid, feats, toks = sizes
    nq, ny = n_dp // 2, n_row
    peers = nq * ny
    pieces = pieces_of(rows)
    dp, y, col = lax.axis_index("dp"), lax.axis_index("row"), lax.axis_index("col")
    q, c = dp // 2, dp % 2
    rep_of = lambda q1, c1, y1: (q1 * 2 + c1) * ny + y1
    at_q = lambda dq: lax.rem(q + dq, nq)
    at_y = lambda dy: lax.rem(y + dy, ny)
    back_q = lambda dq: lax.rem(q + nq - dq, nq)
    back_y = lambda dy: lax.rem(y + ny - dy, ny)
    me = rep_of(q, c, y)
    partner = {"dp": q * 2 + 1 - c}
    q_peer = lambda dq: {"dp": at_q(dq) * 2 + c}
    y_peer = lambda dy: {"row": at_y(dy)}
    xs, ys = [q_peer(i) for i in range(1, nq)], [y_peer(i) for i in range(1, ny)]

    barrier = pltpu.get_barrier_semaphore()
    friends = [partner] + xs + ys
    friends += [{"col": lax.rem(col + i, n_col)} for i in range(1, n_col)]
    for friend in friends:
        pl.semaphore_signal(barrier, inc=1, device_id=friend, device_id_type=MESH)
    pl.semaphore_wait(barrier, len(friends))

    sends = Sends(send_sem)
    mine = (wg_ref, wu_ref, wd_ref)
    streams = (act_ref, cot_ref)

    def rows_at(rep, r0, nr):
        return pl.ds(pl.multiple_of(rep * rows + r0, 8), nr)

    def slot(p, rep):
        w, r0, nr, _ = pieces[p]
        return weights.at[w, rows_at(rep, r0, nr), :]

    half = feats // 2

    def feat_slot(s, h, block):
        return full.at[s, pl.ds(pl.multiple_of(block * feats + h * half, 8), half), :]

    def feat_sem(s, h, block):
        return x_sem.at[(s * 2 + h) * n_col + block]

    has_right, has_left = col < n_col - 1, col > 0
    right = {"col": jnp.minimum(col + 1, n_col - 1)}
    left = {"col": jnp.maximum(col - 1, 0)}

    def own_features(s):
        for h in range(2):
            src = streams[s].at[pl.ds(h * half, half), :]
            sends.start(src, feat_slot(s, h, col), feat_sem(s, h, col), right, has_right)
            sends.start(src, feat_slot(s, h, col), feat_sem(s, h, col), left, has_left)

    def own_piece(p, wheres):
        w, r0, nr, _ = pieces[p]
        for where in wheres:
            sends.start(mine[w].at[pl.ds(r0, nr), :], slot(p, me), w_sem.at[p * peers * 2 + me], where)

    early = [p for p in range(len(pieces)) if pieces[p][0] < 2]
    later = [p for p in range(len(pieces)) if pieces[p][0] == 2]
    own_features(0)
    for p in early:
        own_piece(p, xs)
    for p in reversed(early):
        own_piece(p, ys)
    for p in early:
        own_piece(p, [partner])
    locals_ = []
    for i, (src, dst) in enumerate(
        [(streams[s], full.at[s, pl.ds(pl.multiple_of(col * feats, 8), feats), :]) for s in range(2)]
        + [(mine[w], weights.at[w, rows_at(me, 0, rows), :]) for w in range(3)]
    ):
        locals_.append(pltpu.make_async_copy(src, dst, own_sem.at[i]))
        locals_[-1].start()

    def chain(s, step):
        from_left, from_right = col >= step, col + step < n_col
        lb, rb = jnp.maximum(col - step, 0), jnp.minimum(col + step, n_col - 1)
        for h in range(2):
            l_slot, l_sem = feat_slot(s, h, lb), feat_sem(s, h, lb)
            r_slot, r_sem = feat_slot(s, h, rb), feat_sem(s, h, rb)
            guarded(from_left, lambda: arrived(l_slot, l_sem))
            if step < n_col - 1:
                sends.start(l_slot, l_slot, l_sem, right, from_left & has_right)
            guarded(from_right, lambda: arrived(r_slot, r_sem))
            if step < n_col - 1:
                sends.start(r_slot, r_slot, r_sem, left, from_right & has_left)

    def take(p, rep, forward):
        sem = w_sem.at[p * peers * 2 + rep]
        arrived(slot(p, rep), sem)
        for where in forward + [partner]:
            sends.start(slot(p, rep), slot(p, rep), sem, where)

    def near_first(p):
        if pieces[p][3] == 0:
            for dq in range(1, nq):
                take(p, rep_of(back_q(dq), c, y), ys)
        else:
            for dy in range(1, ny):
                take(p, rep_of(q, c, back_y(dy)), xs)

    def near_rest(p):
        if pieces[p][3] == 0:
            for dy in range(1, ny):
                take(p, rep_of(q, c, back_y(dy)), [])
        else:
            for dq in range(1, nq):
                take(p, rep_of(back_q(dq), c, y), [])

    def far(p):
        for dq in range(1, nq):
            for dy in range(1, ny):
                take(p, rep_of(back_q(dq), c, back_y(dy)), [])

    def from_partner(p):
        for dq in range(nq):
            for dy in range(ny):
                rep = rep_of(at_q(dq), 1 - c, at_y(dy))
                arrived(slot(p, rep), w_sem.at[p * peers * 2 + rep])

    chain(0, 1)
    for p in early:
        near_first(p)
    for p in later:
        own_piece(p, xs)
    for p in reversed(later):
        own_piece(p, ys)
    for p in later:
        own_piece(p, [partner])
    for step in range(2, n_col - 1):
        chain(0, step)
    own_features(1)
    for p in early:
        near_rest(p)
    if n_col > 2:
        chain(0, n_col - 1)
    chain(1, 1)
    for p in early:
        far(p)
    for p in early:
        from_partner(p)
    for copy in locals_:
        copy.wait()

    mt, nt = tile_of(toks, 256), tile_of(hid, 384)
    m_tiles, n_tiles = toks // mt, hid // nt
    token_dims = (((0,), (0,)), ((), ()))

    def tile_slices(i):
        m, n = i // n_tiles, i % n_tiles
        return pl.ds(pl.multiple_of(m * mt, mt), mt), pl.ds(pl.multiple_of(n * nt, nt), nt)

    def project(first, last):
        @pl.loop(first, last)
        def _(i):
            ms, ns = tile_slices(i)
            x = full[0, :, ms]
            gate_pre = lax.dot_general(x, weights[0, :, ns], token_dims, preferred_element_type=F32)
            up_pre = lax.dot_general(x, weights[1, :, ns], token_dims, preferred_element_type=F32)
            act_val, slope_val = gelu_parts(gate_pre)
            grads[2, ms, ns] = (act_val * up_pre).astype(BF16)
            stash[0, ms, ns] = up_pre * slope_val
            stash[1, ms, ns] = act_val

    tiles = m_tiles * n_tiles
    project(0, tiles // 2)
    for p in later:
        near_first(p)
    project(tiles // 2, tiles)

    def n_slice(n):
        return pl.ds(pl.multiple_of(n * nt, nt), nt)

    def term(w, rep, ns):
        return jnp.dot(full[w // 2, rows_at(rep, 0, rows), :], grads[w, :, ns], preferred_element_type=F32)

    def pair_copy(i):
        return pltpu.make_async_remote_copy(
            src_ref=partner_out.at[i],
            dst_ref=sums.at[i],
            send_sem=pair_send.at[i],
            recv_sem=pair_recv.at[i],
            device_id=partner,
            device_id_type=MESH,
        )

    def distance(rep):
        return jnp.abs((rep * rows) // feats - col)

    first_base, count = [], [0, 0]
    for w, _, _, route in pieces:
        first_base.append(count[w // 2])
        count[w // 2] += (nq - 1) * ny if route == 0 else (ny - 1) * nq
    second_base, count = [], [0, 0]
    for w, _, _, route in pieces:
        second_base.append(count[w // 2])
        count[w // 2] += (ny - 1) if route == 0 else (nq - 1)

    def first_slot(p, dq, dy):
        k = first_base[p] + ((dq - 1) * ny + dy if pieces[p][3] == 0 else (dy - 1) * nq + dq)
        late = pieces[p][0] // 2
        return first_in[late].at[k], first_sem[late].at[k]

    def second_slot(p, d):
        k = second_base[p] + d - 1
        late = pieces[p][0] // 2
        return second_in[late].at[k], second_sem[late].at[k]

    def partner_term(w, dq, dy, when=None):
        rep = rep_of(at_q(dq), 1 - c, at_y(dy))
        i = w * peers + at_q(dq) * ny + at_y(dy)

        def one():
            @pl.loop(0, n_tiles)
            def _(n):
                partner_out[i, :, n_slice(n)] = term(w, rep, n_slice(n)).astype(BF16)

            pair_copy(i).start()

        guarded(None if when is None else when(rep), one)

    def own_term(w, dq, dy, when=None):
        index = w * peers + at_q(dq) * ny + at_y(dy)
        rep = rep_of(at_q(dq), c, at_y(dy))
        cond = None if when is None else when(rep)

        def one():
            arrived(sums.at[index], pair_recv.at[index])

            @pl.loop(0, n_tiles)
            def _(n):
                ns = n_slice(n)
                sums[index, :, ns] = (term(w, rep, ns) + sums[index, :, ns].astype(F32)).astype(BF16)

        guarded(cond, one)
        for p, (pw, r0, nr, route) in enumerate(pieces):
            if pw == w and (dq if route == 0 else dy):
                dst, sem = first_slot(p, dq, dy)
                where = q_peer(dq) if route == 0 else y_peer(dy)
                sends.start(sums.at[index, pl.ds(r0, nr), :], dst, sem, where, cond)

    grid_order = [(dq, dy) for dq in others_first(nq) for dy in others_first(ny)]

    def terms(w, when=None, order=grid_order):
        for dq, dy in order:
            partner_term(w, dq, dy, when)
        for dq, dy in order:
            own_term(w, dq, dy, when)

    def second_send(p, when=None):
        w, r0, nr, route = pieces[p]
        rs = pl.ds(r0, nr)
        n_first, n_second = (nq, ny) if route == 0 else (ny, nq)
        for d in range(1, n_second):
            index = w * peers + (q * ny + at_y(d) if route == 0 else at_q(d) * ny + y)
            rep = rep_of(q, c, at_y(d)) if route == 0 else rep_of(at_q(d), c, y)
            cond = None if when is None else when(rep)

            def one():
                total = sums[index, rs, :].astype(F32)
                for f in range(1, n_first):
                    ref, sem = first_slot(p, f, d) if route == 0 else first_slot(p, d, f)
                    arrived(ref, sem)
                    total = total + ref[...].astype(F32)
                sums[index, rs, :] = total.astype(BF16)

            guarded(cond, one)
            dst, sem = second_slot(p, d)
            sends.start(sums.at[index, rs, :], dst, sem, y_peer(d) if route == 0 else q_peer(d), cond)

    def second_own(p):
        w, r0, nr, route = pieces[p]
        rs = pl.ds(r0, nr)
        total = sums[w * peers + q * ny + y, rs, :].astype(F32)
        for f in range(1, nq if route == 0 else ny):
            ref, sem = first_slot(p, f, 0) if route == 0 else first_slot(p, 0, f)
            arrived(ref, sem)
            total = total + ref[...].astype(F32)
        outs[w, rs, :] = total

    out_refs = (og_ref, ou_ref, od_ref)
    leaving = []

    def leave(src, dst):
        leaving.append(pltpu.make_async_copy(src, dst, out_sem.at[len(leaving)]))
        leaving[-1].start()

    def second_final(p):
        w, r0, nr, route = pieces[p]
        rs = pl.ds(r0, nr)
        for d in range(1, ny if route == 0 else nq):
            ref, sem = second_slot(p, d)
            arrived(ref, sem)
            outs[w, rs, :] = outs[w, rs, :] + ref[...].astype(F32)
        leave(outs.at[w, rs, :], out_refs[w].at[rs, :])

    near_rep = lambda rep: distance(rep) <= 1
    for step in range(2, n_col - 1):
        terms(2, (lambda s: lambda rep: distance(rep) == s - 1)(step) if step > 2 else near_rep)
        chain(1, step)
    if n_col > 2:
        terms(2, (lambda rep: distance(rep) == n_col - 2) if n_col > 3 else near_rep)
    far_rep = lambda rep: distance(rep) == n_col - 1
    not_far = lambda rep: distance(rep) < n_col - 1
    for p in later:
        near_rest(p)
    for p in later:
        far(p)
    for p in later:
        from_partner(p)

    rest = n_col - 1
    lo = pl.multiple_of(jnp.where(col == n_col - 1, feats, 0), 32)
    last = pl.multiple_of(jnp.where(col == n_col - 1, 0, rest * feats), 32)

    @pl.loop(0, tiles)
    def _(i):
        ms, ns = tile_slices(i)
        ks = pl.ds(lo, rest * feats)
        acc[ms, ns] = lax.dot_general(full[1, ks, ms], weights[2, ks, ns], token_dims, preferred_element_type=F32)

    for p in later:
        second_send(p, not_far)
    chain(1, n_col - 1)

    @pl.loop(0, tiles)
    def _(i):
        ms, ns = tile_slices(i)
        ks = pl.ds(last, feats)
        hidden_grad = acc[ms, ns] + lax.dot_general(
            full[1, ks, ms], weights[2, ks, ns], token_dims, preferred_element_type=F32)
        grads[0, ms, ns] = (hidden_grad * stash[0, ms, ns]).astype(BF16)
        grads[1, ms, ns] = (hidden_grad * stash[1, ms, ns]).astype(BF16)

    terms(2, far_rep)

    rt = tile_of(feats, 288)
    hid_dims = (((1,), (1,)), ((), ()))
    low = col < n_col // 2
    high = jnp.logical_not(low)

    def ig_part(k, h):
        block = jnp.where(low, n_col - 1 - k, k)
        return ig_out.at[block, pl.ds(h * half, half), :], block

    def ig_slot(going_left, d, h):
        k = (going_left * n_col + d) * 2 + h
        return ig_in.at[going_left * (n_col - 1) + d - (1 - going_left), pl.ds(h * half, half), :], ig_sem.at[k]

    def input_part(k):
        block = jnp.where(low, n_col - 1 - k, k)

        @pl.loop(0, feats // rt)
        def _(r):
            rs = pl.ds(pl.multiple_of(block * feats + r * rt, 8), rt)
            part = lax.dot_general(weights[0, rs, :], grads[0], hid_dims, preferred_element_type=F32)
            part = part + lax.dot_general(weights[1, rs, :], grads[1], hid_dims, preferred_element_type=F32)
            ig_out[block, pl.ds(pl.multiple_of(r * rt, 8), rt), :] = part.astype(BF16)

        if k < n_col - 1:
            for h in range(2):
                src = lambda b: ig_out.at[b, pl.ds(h * half, half), :]
                dst, sem = ig_slot(0, n_col - 1 - k, h)
                sends.start(src(n_col - 1 - k), dst, sem, right, col == 0)
                dst, sem = ig_slot(1, k, h)
                sends.start(src(k), dst, sem, left, col == n_col - 1)

    def relay(going_left, k, side=None):
        d = k if going_left else n_col - 1 - k
        inside = (col > d) & (col < n_col - 1) if going_left else (col < d) & (col > 0)
        if side is not None:
            inside = inside & side
        for h in range(2):
            ref, sem = ig_slot(going_left, d, h)
            part = ig_out.at[d, pl.ds(h * half, half), :]

            def one():
                arrived(ref, sem)
                part[...] = (part[...].astype(F32) + ref[...].astype(F32)).astype(BF16)

            guarded(inside, one)
            sends.start(part, ref, sem, left if going_left else right, inside)

    first_off = grid_order[0]
    split = lambda route: [g for g in grid_order if (g[0] if route == 0 else g[1])]
    stay = lambda route: [g for g in grid_order if not (g[0] if route == 0 else g[1])]
    sent = [split(0), split(1)]
    for i in range(max(len(sent[0]), len(sent[1]))):
        for w in range(2):
            if i < len(sent[w]):
                partner_term(w, *sent[w][i])
        for w in range(2):
            if i < len(sent[w]):
                own_term(w, *sent[w][i])
        if i == 0:
            input_part(0)
    for p in later:
        second_send(p, far_rep)
    for k in range(1, n_col - 1):
        input_part(k)
    for w in range(2):
        terms(w, None, stay(w))
    input_part(n_col - 1)
    relay(0, 0, low)
    relay(1, 0, high)
    for p in early:
        second_send(p)
    for p in later:
        second_own(p)
    for p in later:
        second_final(p)
    for k in range(1, n_col - 1):
        relay(0, k, low)
        relay(1, k, high)
    for k in range(n_col - 1):
        relay(1, k, low)
        relay(0, k, high)
    for p in early:
        second_own(p)

    for h in range(2):
        hs = pl.ds(h * half, half)
        from_left, left_sem = ig_slot(0, jnp.maximum(col, 1), h)
        from_right, right_sem = ig_slot(1, jnp.minimum(col, n_col - 2), h)
        guarded(has_left, lambda: arrived(from_left, left_sem))
        guarded(has_right, lambda: arrived(from_right, right_sem))
        own = ig_out[col, hs, :].astype(F32)

        @pl.when(has_left & has_right)
        def _():
            ig_out[col, hs, :] = (own + from_left[...].astype(F32) + from_right[...].astype(F32)).astype(BF16)

        @pl.when(jnp.logical_not(has_left))
        def _():
            ig_out[col, hs, :] = (own + from_right[...].astype(F32)).astype(BF16)

        @pl.when(jnp.logical_not(has_right))
        def _():
            ig_out[col, hs, :] = (own + from_left[...].astype(F32)).astype(BF16)

        leave(ig_out.at[col, hs, :], ig_ref.at[hs, :])
    for p in early:
        second_final(p)
    sends.finish()
    for copy in leaving:
        copy.wait()

    @pl.loop(0, 3 * peers)
    def _(i):
        pair_copy(i).wait_send()


def body(n_dp, n_row, n_col, act_in, cot_out, w_gate, w_up, w_down):
    toks, feats = act_in.shape
    rows, hid = w_gate.shape
    sizes = (n_dp, n_row, n_col, rows, hid, feats, toks)
    nq, ny = n_dp // 2, n_row
    peers, reps, dim = nq * ny, n_dp * n_row, feats * n_col
    pieces = pieces_of(rows)
    firsts, seconds = [0, 0], [0, 0]
    for w, _, _, route in pieces:
        firsts[w // 2] += (nq - 1) * ny if route == 0 else (ny - 1) * nq
        seconds[w // 2] += (ny - 1) if route == 0 else (nq - 1)
    n_pieces = len(pieces)
    n_sends = 8 + 8 * (n_col - 2) + n_pieces * (nq + ny - 1) + n_pieces * (peers - 1) * max(nq, ny)
    n_sends += sum(firsts) * 2 + sum(seconds) * 4 + 4 * (n_col - 1) + 8 * n_col * 3
    late_rows = min(nr for w, _, nr, _ in pieces if w == 2)
    any_spec = pl.BlockSpec(memory_space=pl.ANY)
    dma = lambda n: pltpu.SemaphoreType.DMA((max(n, 1),))
    landing = lambda n: [pltpu.VMEM((max(n[0], 1), rows, hid), BF16), pltpu.VMEM((max(n[1], 1), late_rows, hid), BF16)]
    wgrad = jax.ShapeDtypeStruct((rows, hid), F32)
    ig_t, gate_grad, up_grad, down_t = pl.pallas_call(
        functools.partial(kernel, sizes),
        out_shape=[jax.ShapeDtypeStruct((feats, toks), BF16), wgrad, wgrad, wgrad],
        in_specs=[any_spec] * 5,
        out_specs=[any_spec] * 4,
        scratch_shapes=[
            pltpu.VMEM((2, dim, toks), BF16),
            pltpu.VMEM((3, dim, hid), BF16),
            pltpu.VMEM((3, toks, hid), BF16),
            pltpu.VMEM((2, toks, hid), F32),
            pltpu.VMEM((toks, hid), F32),
            pltpu.VMEM((3 * peers, rows, hid), BF16),
            pltpu.VMEM((3 * peers, rows, hid), BF16),
            landing(firsts),
            landing(seconds),
            pltpu.VMEM((n_col, feats, toks), BF16),
            pltpu.VMEM((2 * (n_col - 1), feats, toks), BF16),
            pltpu.VMEM((3, rows, hid), F32),
            dma(5), dma(n_sends), dma(n_pieces * reps), dma(4 * n_col), dma(3 * peers), dma(3 * peers),
            [dma(n) for n in firsts], [dma(n) for n in seconds], dma(4 * n_col), dma(n_pieces + 2),
        ],
        compiler_params=pltpu.CompilerParams(
            collective_id=0, has_side_effects=True, vmem_limit_bytes=67043328
        ),
    )(act_in.T, cot_out.T, w_gate, w_up, w_down.T)
    norm_scale = 1.0 / math.sqrt(toks * n_dp * n_row)
    return (ig_t.T, gate_grad * norm_scale, up_grad * norm_scale, (down_t * norm_scale).T)


def solution(mesh):
    grid = P(("dp", "row"), "col")
    flipped = P("col", ("dp", "row"))
    return jax.shard_map(
        functools.partial(body, mesh.shape["dp"], mesh.shape["row"], mesh.shape["col"]),
        mesh=mesh,
        in_specs=(grid, grid, grid, grid, flipped),
        out_specs=(grid, grid, grid, flipped),
        check_vma=False,
    )
```

time: 170 us -> 156 us (0.918)
  Pallas kernels: 162 us -> 147 us
    pallas_call x1, Pallas kernels: 162 us -> 147 us  [body(): pl.pallas_call(functools.partial(kernel, sizes), out_shape=[jax.ShapeDtyp...]
where the time goes in v1:
time: 156 us; the launch traced here: 153 us
  Pallas kernels  147 us (94%)
  other arithmetic  4.29 us (3%)
    pallas_call x1, Pallas kernels, body(): pl.pallas_call(functools.partial(kernel, sizes), out_shape=[jax.ShapeDtyp...  147 us

profile of v1, /device:TPU:5, one launch (start us, length us, event | category | flops | bytes accessed | tf_op | source)
XLA Modules:
  0.0 152.9 jit_solution(4251729239732374035)
XLA Ops:
  0.6 147.2 %shard_map.84 = (bf16[576,512]{1,0:T(8,128)(2,1)}, f32[288,1152]{1,0:T(8,128)}, f32[288,1152]{1,0:T(8,128)}, f32[288,1152]{1,0:T(8,128)}) custom-call(bf16[576,512]{1,0:T(8,128)(2,1)} %bitcast.8, bf16[576,512]{1,0:T(8,128)(2,1)} %bitcast.9, bf16[288,1152]{1,0:T(8,128)(2,1)} %wg_ref.1, bf16[288,1152]{1,0:T(8,128)(2,1)} %wu_ref.1, bf16[288,1152]{1,0:T(8,128)(2,1)} %bitcast.6), custom_call_target="tpu_custom_call" | custom-call | tf_op jit(solution)/shard_map/pallas_call | solution.py:550
  147.8 0.0 copy-start
  147.8 0.0 copy-start.1
  147.8 2.6 %broadcast_multiply_fusion.1 = f32[288,1152]{1,0:T(8,128)} fusion(f32[288,1152]{1,0:T(8,128)} %get-tuple-element.9), kind=kLoop, calls=%fused_computation.2 | loop fusion | flops 331776 | bytes 2654208 | tf_op jit(solution)/shard_map/mul | solution.py:576
  150.4 0.0 copy-done
  150.4 0.0 copy-done.1
  150.4 0.0 copy-start.2
  150.4 1.7 %multiply_bitcast_fusion = (f32[1152,288]{0,1:T(8,128)}, f32[288,1152]{1,0:T(8,128)}) fusion(f32[288,1152]{1,0:T(8,128)S(1)} %copy-done.1, f32[288,1152]{1,0:T(8,128)S(1)} %copy-done), kind=kLoop, calls=%fused_computation | loop fusion | flops 663552 | bytes 5308416 | tf_op jit(solution)/shard_map/transpose | solution.py:576
  152.1 0.0 copy-done.2
  152.1 0.8 copy.10
Async XLA Ops:
  147.8 2.6 %copy-start = (f32[288,1152]{1,0:T(8,128)S(1)}, f32[288,1152]{1,0:T(8,128)}, u32[]{:S(2)}) copy-start(f32[288,1152]{1,0:T(8,128)} %get-tuple-element.10) | copy-start | bytes 3981316
  147.8 2.6 %copy-start.1 = (f32[288,1152]{1,0:T(8,128)S(1)}, f32[288,1152]{1,0:T(8,128)}, u32[]{:S(2)}) copy-start(f32[288,1152]{1,0:T(8,128)} %get-tuple-element.11) | copy-start | bytes 3981316
  150.4 1.7 %copy-start.2 = (bf16[576,512]{1,0:T(8,128)(2,1)S(1)}, bf16[576,512]{1,0:T(8,128)(2,1)}, u32[]{:S(2)}) copy-start(bf16[576,512]{1,0:T(8,128)(2,1)} %get-tuple-element.8) | copy-start | bytes 1769476

commit v2 on v1

--- a/solution.py
+++ b/solution.py
@@ -73,8 +73,8 @@
 
 
 def kernel(sizes, act_ref, cot_ref, wg_ref, wu_ref, wd_ref, ig_ref, og_ref, ou_ref, od_ref,
-           full, weights, grads, stash, acc, partner_out, sums, first_in, second_in, ig_out, ig_in, outs,
-           own_sem, send_sem, w_sem, x_sem, pair_send, pair_recv, first_sem, second_sem, ig_sem, out_sem):
+           full, weights, grads, stash, acc, partner_out, sums, first_in, second_in, ig_out, ig_in,
+           own_sem, send_sem, w_sem, x_sem, pair_send, pair_recv, first_sem, second_sem, ig_sem, slice_sem):
     n_dp, n_row, n_col, rows, hid, feats, toks = sizes
     nq, ny = n_dp // 2, n_row
     peers = nq * ny
@@ -94,10 +94,16 @@
 
     barrier = pltpu.get_barrier_semaphore()
     friends = [partner] + xs + ys
-    friends += [{"col": lax.rem(col + i, n_col)} for i in range(1, n_col)]
     for friend in friends:
         pl.semaphore_signal(barrier, inc=1, device_id=friend, device_id_type=MESH)
-    pl.semaphore_wait(barrier, len(friends))
+    has_right, has_left = col < n_col - 1, col > 0
+    right = {"col": jnp.minimum(col + 1, n_col - 1)}
+    left = {"col": jnp.maximum(col - 1, 0)}
+    for there, friend in ((has_right, right), (has_left, left)):
+        @pl.when(there)
+        def _():
+            pl.semaphore_signal(barrier, inc=1, device_id=friend, device_id_type=MESH)
+    pl.semaphore_wait(barrier, len(friends) + has_right.astype(jnp.int32) + has_left.astype(jnp.int32))
 
     sends = Sends(send_sem)
     mine = (wg_ref, wu_ref, wd_ref)
@@ -118,15 +124,17 @@
     def feat_sem(s, h, block):
         return x_sem.at[(s * 2 + h) * n_col + block]
 
-    has_right, has_left = col < n_col - 1, col > 0
-    right = {"col": jnp.minimum(col + 1, n_col - 1)}
-    left = {"col": jnp.maximum(col - 1, 0)}
-
-    def own_features(s):
-        for h in range(2):
+    at_end = (col == 0) | (col == n_col - 1)
+    middle = jnp.logical_not(at_end)
+    low = col < n_col // 2
+    high = jnp.logical_not(low)
+    staggered = n_col == 4 and nq == 2 and rows == half
+
+    def own_features(s, to_right, to_left, halves=range(2)):
+        for h in halves:
             src = streams[s].at[pl.ds(h * half, half), :]
-            sends.start(src, feat_slot(s, h, col), feat_sem(s, h, col), right, has_right)
-            sends.start(src, feat_slot(s, h, col), feat_sem(s, h, col), left, has_left)
+            sends.start(src, feat_slot(s, h, col), feat_sem(s, h, col), right, to_right)
+            sends.start(src, feat_slot(s, h, col), feat_sem(s, h, col), left, to_left)
 
     def own_piece(p, wheres):
         w, r0, nr, _ = pieces[p]
@@ -135,7 +143,8 @@
 
     early = [p for p in range(len(pieces)) if pieces[p][0] < 2]
     later = [p for p in range(len(pieces)) if pieces[p][0] == 2]
-    own_features(0)
+    own_features(0, has_right, has_left)
+    own_features(1, has_right & at_end, has_left & at_end)
     for p in early:
         own_piece(p, xs)
     for p in reversed(early):
@@ -150,8 +159,8 @@
         locals_.append(pltpu.make_async_copy(src, dst, own_sem.at[i]))
         locals_[-1].start()
 
-    def chain(s, step):
-        from_left, from_right = col >= step, col + step < n_col
+    def chain(s, step, when_left, when_right):
+        from_left, from_right = (col >= step) & when_left, (col + step < n_col) & when_right
         lb, rb = jnp.maximum(col - step, 0), jnp.minimum(col + step, n_col - 1)
         for h in range(2):
             l_slot, l_sem = feat_slot(s, h, lb), feat_sem(s, h, lb)
@@ -163,6 +172,14 @@
             if step < n_col - 1:
                 sends.start(r_slot, r_slot, r_sem, left, from_right & has_left)
 
+    late_end = at_end if staggered else col < 0
+    late_mid = middle if staggered else col < 0
+
+    def end_wait(d, halves, when):
+        block = jnp.where(low, d, n_col - 1 - d)
+        for h in halves:
+            guarded(at_end & when, lambda: arrived(feat_slot(1, h, block), feat_sem(1, h, block)))
+
     def take(p, rep, forward):
         sem = w_sem.at[p * peers * 2 + rep]
         arrived(slot(p, rep), sem)
@@ -196,7 +213,10 @@
                 rep = rep_of(at_q(dq), 1 - c, at_y(dy))
                 arrived(slot(p, rep), w_sem.at[p * peers * 2 + rep])
 
-    chain(0, 1)
+    always = col >= 0
+    chain(0, 1, always, always)
+    if n_col == 4:
+        own_features(1, middle & low, middle & high)
     for p in early:
         near_first(p)
     for p in later:
@@ -206,13 +226,22 @@
     for p in later:
         own_piece(p, [partner])
     for step in range(2, n_col - 1):
-        chain(0, step)
-    own_features(1)
+        chain(0, step, always, always)
+    prompt = jnp.logical_not(late_mid)
+    if n_col == 4:
+        own_features(1, middle & high, middle & low, [0])
+        own_features(1, middle & high & prompt, middle & low & prompt, [1])
+        chain(1, 1, middle & low, middle & high)
+    else:
+        own_features(1, middle, middle)
     for p in early:
         near_rest(p)
     if n_col > 2:
-        chain(0, n_col - 1)
-    chain(1, 1)
+        chain(0, n_col - 1, always, always)
+    if n_col == 4:
+        chain(1, 1, middle & high, middle & low)
+    else:
+        chain(1, 1, middle, middle)
     for p in early:
         far(p)
     for p in early:
@@ -244,17 +273,18 @@
     project(0, tiles // 2)
     for p in later:
         near_first(p)
+    for step in range(2, n_col - 1):
+        chain(1, step, middle, middle)
+    if staggered:
+        own_features(1, middle & high & late_mid, middle & low & late_mid, [1])
     project(tiles // 2, tiles)
 
-    def n_slice(n):
-        return pl.ds(pl.multiple_of(n * nt, nt), nt)
-
-    def term(w, rep, ns):
-        return jnp.dot(full[w // 2, rows_at(rep, 0, rows), :], grads[w, :, ns], preferred_element_type=F32)
+    def term(w, rep):
+        return jnp.dot(full[w // 2, rows_at(rep, 0, rows), :], grads[w], preferred_element_type=F32)
 
     def pair_copy(i):
         return pltpu.make_async_remote_copy(
-            src_ref=partner_out.at[i],
+            src_ref=partner_out.at[lax.rem(i, 2 * peers)],
             dst_ref=sums.at[i],
             send_sem=pair_send.at[i],
             recv_sem=pair_recv.at[i],
@@ -262,8 +292,23 @@
             device_id_type=MESH,
         )
 
-    def distance(rep):
-        return jnp.abs((rep * rows) // feats - col)
+    last_stage = max(n_col - 2, 0)
+
+    def stage_of(rep, late):
+        block = (rep * rows) // feats
+        dist = jnp.abs(block - col)
+        plain = jnp.maximum(dist - 1, 0)
+        if not staggered:
+            return plain
+        second_half = lax.rem(rep, feats // rows) == 1
+        shifted = jnp.where(dist == 1, jnp.where(second_half, 2, 0), jnp.maximum(dist - 2, 0))
+        return jnp.where(late, shifted, plain)
+
+    def own_stage(rep):
+        return stage_of(rep, late_end)
+
+    def sum_stage(rep, route):
+        return own_stage(rep)
 
     first_base, count = [], [0, 0]
     for w, _, _, route in pieces:
@@ -289,41 +334,57 @@
         i = w * peers + at_q(dq) * ny + at_y(dy)
 
         def one():
-            @pl.loop(0, n_tiles)
-            def _(n):
-                partner_out[i, :, n_slice(n)] = term(w, rep, n_slice(n)).astype(BF16)
-
+            if w == 0:
+                pair_copy(2 * peers + i).wait_send()
+            partner_out[lax.rem(i, 2 * peers)] = term(w, rep).astype(BF16)
             pair_copy(i).start()
 
         guarded(None if when is None else when(rep), one)
+
+    def slice_copy(p, dq, dy):
+        w, r0, nr, route = pieces[p]
+        index = w * peers + at_q(dq) * ny + at_y(dy)
+        dst, sem = first_slot(p, dq, dy)
+        return pltpu.make_async_remote_copy(
+            src_ref=sums.at[index, pl.ds(r0, nr), :],
+            dst_ref=dst,
+            send_sem=slice_sem.at[p * peers + dq * ny + dy],
+            recv_sem=sem,
+            device_id=q_peer(dq) if route == 0 else y_peer(dy),
+            device_id_type=MESH,
+        )
 
     def own_term(w, dq, dy, when=None):
         index = w * peers + at_q(dq) * ny + at_y(dy)
         rep = rep_of(at_q(dq), c, at_y(dy))
-        cond = None if when is None else when(rep)
 
         def one():
             arrived(sums.at[index], pair_recv.at[index])
-
-            @pl.loop(0, n_tiles)
-            def _(n):
-                ns = n_slice(n)
-                sums[index, :, ns] = (term(w, rep, ns) + sums[index, :, ns].astype(F32)).astype(BF16)
-
-        guarded(cond, one)
-        for p, (pw, r0, nr, route) in enumerate(pieces):
-            if pw == w and (dq if route == 0 else dy):
-                dst, sem = first_slot(p, dq, dy)
-                where = q_peer(dq) if route == 0 else y_peer(dy)
-                sends.start(sums.at[index, pl.ds(r0, nr), :], dst, sem, where, cond)
+            sums[index] = (term(w, rep) + sums[index].astype(F32)).astype(BF16)
+            for p, (pw, _, _, route) in enumerate(pieces):
+                if pw == w:
+                    away = dq if route == 0 else dy
+                    if not isinstance(away, int):
+                        pl.when(away > 0)(slice_copy(p, dq, dy).start)
+                    elif away:
+                        slice_copy(p, dq, dy).start()
+
+        guarded(None if when is None else when(rep), one)
 
     grid_order = [(dq, dy) for dq in others_first(nq) for dy in others_first(ny)]
 
-    def terms(w, when=None, order=grid_order):
-        for dq, dy in order:
-            partner_term(w, dq, dy, when)
-        for dq, dy in order:
-            own_term(w, dq, dy, when)
+    def place(i):
+        return lax.rem(1 + i // ny, nq), lax.rem(1 + i % ny, ny)
+
+    def partner_terms(w, when=None):
+        @pl.loop(0, peers)
+        def _(i):
+            partner_term(w, *place(i), when)
+
+    def own_terms(w, when=None):
+        @pl.loop(0, peers)
+        def _(i):
+            own_term(w, *place(i), when)
 
     def second_send(p, when=None):
         w, r0, nr, route = pieces[p]
@@ -332,7 +393,7 @@
         for d in range(1, n_second):
             index = w * peers + (q * ny + at_y(d) if route == 0 else at_q(d) * ny + y)
             rep = rep_of(q, c, at_y(d)) if route == 0 else rep_of(at_q(d), c, y)
-            cond = None if when is None else when(rep)
+            cond = None if when is None else when(sum_stage(rep, route))
 
             def one():
                 total = sums[index, rs, :].astype(F32)
@@ -345,6 +406,8 @@
             guarded(cond, one)
             dst, sem = second_slot(p, d)
             sends.start(sums.at[index, rs, :], dst, sem, y_peer(d) if route == 0 else q_peer(d), cond)
+
+    outs = (og_ref, ou_ref, od_ref)
 
     def second_own(p):
         w, r0, nr, route = pieces[p]
@@ -354,14 +417,7 @@
             ref, sem = first_slot(p, f, 0) if route == 0 else first_slot(p, 0, f)
             arrived(ref, sem)
             total = total + ref[...].astype(F32)
-        outs[w, rs, :] = total
-
-    out_refs = (og_ref, ou_ref, od_ref)
-    leaving = []
-
-    def leave(src, dst):
-        leaving.append(pltpu.make_async_copy(src, dst, out_sem.at[len(leaving)]))
-        leaving[-1].start()
+        outs[w][rs, :] = total
 
     def second_final(p):
         w, r0, nr, route = pieces[p]
@@ -369,57 +425,71 @@
         for d in range(1, ny if route == 0 else nq):
             ref, sem = second_slot(p, d)
             arrived(ref, sem)
-            outs[w, rs, :] = outs[w, rs, :] + ref[...].astype(F32)
-        leave(outs.at[w, rs, :], out_refs[w].at[rs, :])
-
-    near_rep = lambda rep: distance(rep) <= 1
-    for step in range(2, n_col - 1):
-        terms(2, (lambda s: lambda rep: distance(rep) == s - 1)(step) if step > 2 else near_rep)
-        chain(1, step)
-    if n_col > 2:
-        terms(2, (lambda rep: distance(rep) == n_col - 2) if n_col > 3 else near_rep)
-    far_rep = lambda rep: distance(rep) == n_col - 1
-    not_far = lambda rep: distance(rep) < n_col - 1
-    for p in later:
-        near_rest(p)
-    for p in later:
-        far(p)
+            outs[w][rs, :] = outs[w][rs, :] + ref[...].astype(F32)
+
+    stage_is = lambda k: lambda rep: own_stage(rep) == k
+    on_time = jnp.logical_not(late_end)
+    for k in range(last_stage):
+        if k == 0:
+            end_wait(1, range(2), on_time)
+            if staggered:
+                end_wait(1, [0], late_end)
+                end_wait(2, range(2), late_end)
+        else:
+            end_wait(k + 1, range(2), on_time)
+            if staggered:
+                end_wait(k + 2, range(2), late_end)
+        partner_terms(2, stage_is(k))
+        own_terms(2, stage_is(k))
+        if k == 0:
+            for p in later:
+                near_rest(p)
+            for p in later:
+                far(p)
     for p in later:
         from_partner(p)
 
-    rest = n_col - 1
-    lo = pl.multiple_of(jnp.where(col == n_col - 1, feats, 0), 32)
-    last = pl.multiple_of(jnp.where(col == n_col - 1, 0, rest * feats), 32)
-
-    @pl.loop(0, tiles)
-    def _(i):
-        ms, ns = tile_slices(i)
-        ks = pl.ds(lo, rest * feats)
-        acc[ms, ns] = lax.dot_general(full[1, ks, ms], weights[2, ks, ns], token_dims, preferred_element_type=F32)
-
-    for p in later:
-        second_send(p, not_far)
-    chain(1, n_col - 1)
-
-    @pl.loop(0, tiles)
-    def _(i):
-        ms, ns = tile_slices(i)
+    inner = max(n_col - 2, 0) * feats
+    single = pl.multiple_of(jnp.where(low, 0, n_col - 1) * feats, 32)
+    pair = pl.multiple_of(jnp.where(late_end, jnp.where(low, 2, 0), 1) * feats, 32)
+    last = pl.multiple_of(
+        jnp.where(late_end, jnp.where(low, 1, n_col - 2), jnp.where(low, n_col - 1, 0)) * feats, 32)
+
+    @pl.loop(0, m_tiles)
+    def _(m):
+        ms = pl.ds(pl.multiple_of(m * mt, mt), mt)
+        ks = pl.ds(single, feats)
+        part = lax.dot_general(full[1, ks, ms], weights[2, ks, :], token_dims, preferred_element_type=F32)
+        if inner:
+            ks = pl.ds(pair, inner)
+            part = part + lax.dot_general(full[1, ks, ms], weights[2, ks, :], token_dims, preferred_element_type=F32)
+        acc[ms, :] = part
+
+    for p in later:
+        second_send(p, lambda k: k < last_stage - 1)
+    end_wait(n_col - 1, range(2), on_time)
+    if staggered:
+        end_wait(1, [1], late_end)
+    partner_terms(2, stage_is(last_stage))
+
+    @pl.loop(0, m_tiles)
+    def _(m):
+        ms = pl.ds(pl.multiple_of(m * mt, mt), mt)
         ks = pl.ds(last, feats)
-        hidden_grad = acc[ms, ns] + lax.dot_general(
-            full[1, ks, ms], weights[2, ks, ns], token_dims, preferred_element_type=F32)
-        grads[0, ms, ns] = (hidden_grad * stash[0, ms, ns]).astype(BF16)
-        grads[1, ms, ns] = (hidden_grad * stash[1, ms, ns]).astype(BF16)
-
-    terms(2, far_rep)
+        acc[ms, :] = acc[ms, :] + lax.dot_general(
+            full[1, ks, ms], weights[2, ks, :], token_dims, preferred_element_type=F32)
+
+    et = tile_of(toks, 32)
+
+    @pl.loop(0, toks // et)
+    def _(m):
+        ms = pl.ds(pl.multiple_of(m * et, et), et)
+        hidden_grad = acc[ms, :]
+        grads[0, ms, :] = (hidden_grad * stash[0, ms, :]).astype(BF16)
+        grads[1, ms, :] = (hidden_grad * stash[1, ms, :]).astype(BF16)
 
     rt = tile_of(feats, 288)
     hid_dims = (((1,), (1,)), ((), ()))
-    low = col < n_col // 2
-    high = jnp.logical_not(low)
-
-    def ig_part(k, h):
-        block = jnp.where(low, n_col - 1 - k, k)
-        return ig_out.at[block, pl.ds(h * half, half), :], block
 
     def ig_slot(going_left, d, h):
         k = (going_left * n_col + d) * 2 + h
@@ -459,34 +529,39 @@
             guarded(inside, one)
             sends.start(part, ref, sem, left if going_left else right, inside)
 
-    first_off = grid_order[0]
-    split = lambda route: [g for g in grid_order if (g[0] if route == 0 else g[1])]
-    stay = lambda route: [g for g in grid_order if not (g[0] if route == 0 else g[1])]
-    sent = [split(0), split(1)]
+    sent = [[g for g in grid_order if g[0]], [g for g in grid_order if g[1]]]
     for i in range(max(len(sent[0]), len(sent[1]))):
-        for w in range(2):
-            if i < len(sent[w]):
-                partner_term(w, *sent[w][i])
-        for w in range(2):
-            if i < len(sent[w]):
-                own_term(w, *sent[w][i])
+        both = [(w, sent[w][i]) for w in range(2) if i < len(sent[w])]
+        for w, place_i in both:
+            partner_term(w, *place_i)
         if i == 0:
+            own_terms(2, stage_is(last_stage))
+        for w, place_i in both:
+            own_term(w, *place_i)
+        if i == 0:
+            for p in later:
+                second_send(p, lambda k: k == last_stage - 1)
             input_part(0)
     for p in later:
-        second_send(p, far_rep)
+        second_send(p, lambda k: k == last_stage)
     for k in range(1, n_col - 1):
         input_part(k)
     for w in range(2):
-        terms(w, None, stay(w))
+        @pl.loop(0, peers // (nq if w == 0 else ny))
+        def _(i):
+            j = lax.rem(i + 1, ny if w == 0 else nq)
+            partner_term(w, *((0, j) if w == 0 else (j, 0)))
+
+        @pl.loop(0, peers // (nq if w == 0 else ny))
+        def _(i):
+            j = lax.rem(i + 1, ny if w == 0 else nq)
+            own_term(w, *((0, j) if w == 0 else (j, 0)))
+
     input_part(n_col - 1)
     relay(0, 0, low)
     relay(1, 0, high)
     for p in early:
         second_send(p)
-    for p in later:
-        second_own(p)
-    for p in later:
-        second_final(p)
     for k in range(1, n_col - 1):
         relay(0, k, low)
         relay(1, k, high)
@@ -495,6 +570,10 @@
         relay(0, k, high)
     for p in early:
         second_own(p)
+    for p in later:
+        second_own(p)
+    for p in later:
+        second_final(p)
 
     for h in range(2):
         hs = pl.ds(h * half, half)
@@ -506,26 +585,29 @@
 
         @pl.when(has_left & has_right)
         def _():
-            ig_out[col, hs, :] = (own + from_left[...].astype(F32) + from_right[...].astype(F32)).astype(BF16)
+            ig_ref[hs, :] = (own + from_left[...].astype(F32) + from_right[...].astype(F32)).astype(BF16)
 
         @pl.when(jnp.logical_not(has_left))
         def _():
-            ig_out[col, hs, :] = (own + from_right[...].astype(F32)).astype(BF16)
+            ig_ref[hs, :] = (own + from_right[...].astype(F32)).astype(BF16)
 
         @pl.when(jnp.logical_not(has_right))
         def _():
-            ig_out[col, hs, :] = (own + from_left[...].astype(F32)).astype(BF16)
-
-        leave(ig_out.at[col, hs, :], ig_ref.at[hs, :])
+            ig_ref[hs, :] = (own + from_left[...].astype(F32)).astype(BF16)
+
     for p in early:
         second_final(p)
     sends.finish()
-    for copy in leaving:
-        copy.wait()
-
-    @pl.loop(0, 3 * peers)
+
+    @pl.loop(0, 2 * peers)
     def _(i):
         pair_copy(i).wait_send()
+
+    for p, (_, _, _, route) in enumerate(pieces):
+        @pl.loop(0, peers)
+        def _(i):
+            dq, dy = i // ny, i % ny
+            pl.when((dq if route == 0 else dy) > 0)(slice_copy(p, dq, dy).wait_send)
 
 
 def body(n_dp, n_row, n_col, act_in, cot_out, w_gate, w_up, w_down):
@@ -540,36 +622,36 @@
         firsts[w // 2] += (nq - 1) * ny if route == 0 else (ny - 1) * nq
         seconds[w // 2] += (ny - 1) if route == 0 else (nq - 1)
     n_pieces = len(pieces)
-    n_sends = 8 + 8 * (n_col - 2) + n_pieces * (nq + ny - 1) + n_pieces * (peers - 1) * max(nq, ny)
+    n_sends = 24 + 8 * n_col + n_pieces * (nq + ny - 1) + n_pieces * (peers - 1) * max(nq, ny)
     n_sends += sum(firsts) * 2 + sum(seconds) * 4 + 4 * (n_col - 1) + 8 * n_col * 3
     late_rows = min(nr for w, _, nr, _ in pieces if w == 2)
     any_spec = pl.BlockSpec(memory_space=pl.ANY)
     dma = lambda n: pltpu.SemaphoreType.DMA((max(n, 1),))
     landing = lambda n: [pltpu.VMEM((max(n[0], 1), rows, hid), BF16), pltpu.VMEM((max(n[1], 1), late_rows, hid), BF16)]
-    wgrad = jax.ShapeDtypeStruct((rows, hid), F32)
+    wgrad = pltpu.VMEM((rows, hid), F32)
     ig_t, gate_grad, up_grad, down_t = pl.pallas_call(
         functools.partial(kernel, sizes),
-        out_shape=[jax.ShapeDtypeStruct((feats, toks), BF16), wgrad, wgrad, wgrad],
+        out_shape=[pltpu.VMEM((feats, toks), BF16), wgrad, wgrad, wgrad],
         in_specs=[any_spec] * 5,
-        out_specs=[any_spec] * 4,
+        out_specs=[pl.BlockSpec(memory_space=pltpu.VMEM)] * 4,
         scratch_shapes=[
             pltpu.VMEM((2, dim, toks), BF16),
             pltpu.VMEM((3, dim, hid), BF16),
             pltpu.VMEM((3, toks, hid), BF16),
             pltpu.VMEM((2, toks, hid), F32),
             pltpu.VMEM((toks, hid), F32),
-            pltpu.VMEM((3 * peers, rows, hid), BF16),
+            pltpu.VMEM((2 * peers, rows, hid), BF16),
             pltpu.VMEM((3 * peers, rows, hid), BF16),
             landing(firsts),
             landing(seconds),
             pltpu.VMEM((n_col, feats, toks), BF16),
             pltpu.VMEM((2 * (n_col - 1), feats, toks), BF16),
-            pltpu.VMEM((3, rows, hid), F32),
             dma(5), dma(n_sends), dma(n_pieces * reps), dma(4 * n_col), dma(3 * peers), dma(3 * peers),
-            [dma(n) for n in firsts], [dma(n) for n in seconds], dma(4 * n_col), dma(n_pieces + 2),
+            [dma(n) for n in firsts], [dma(n) for n in seconds], dma(4 * n_col),
+            dma(n_pieces * peers),
         ],
         compiler_params=pltpu.CompilerParams(
-            collective_id=0, has_side_effects=True, vmem_limit_bytes=67043328
+            collective_id=0, has_side_effects=True, vmem_limit_bytes=60600000
         ),
     )(act_in.T, cot_out.T, w_gate, w_up, w_down.T)
     norm_scale = 1.0 / math.sqrt(toks * n_dp * n_row)

time: 156 us -> 146 us (0.936); the launches traced: 153 us -> 146 us
  Pallas kernels: 147 us -> 142 us
    pallas_call x1, Pallas kernels: 147 us -> 142 us  [body(): pl.pallas_call(functools.partial(kernel, sizes), out_shape=[pltpu.VMEM((f...]
where the time goes in v2:
time: 146 us
  Pallas kernels  142 us (97%)
  other arithmetic  2.82 us (2%)
    pallas_call x1, Pallas kernels, body(): pl.pallas_call(functools.partial(kernel, sizes), out_shape=[pltpu.VMEM((f...  142 us

profile of v2, /device:TPU:5, one launch (start us, length us, event | category | flops | bytes accessed | tf_op | source)
XLA Modules:
  0.0 145.8 jit_solution(3570504299359335692)
XLA Ops:
  0.6 141.6 %shard_map.84 = (bf16[576,512]{1,0:T(8,128)(2,1)S(1)}, f32[288,1152]{1,0:T(8,128)S(1)}, f32[288,1152]{1,0:T(8,128)S(1)}, f32[288,1152]{1,0:T(8,128)S(1)}) custom-call(bf16[576,512]{1,0:T(8,128)(2,1)} %bitcast.8, bf16[576,512]{1,0:T(8,128)(2,1)} %bitcast.9, bf16[288,1152]{1,0:T(8,128)(2,1)} %wg_ref.1, bf16[288,1152]{1,0:T(8,128)(2,1)} %wu_ref.1, ...), custom_call_target="tpu_custom_call" | custom-call | tf_op jit(solution)/shard_map/pallas_call | solution.py:632
  142.2 0.8 copy.10
  143.0 1.1 broadcast_multiply_fusion.1
  144.2 1.7 %multiply_bitcast_fusion = (f32[1152,288]{0,1:T(8,128)}, f32[288,1152]{1,0:T(8,128)}) fusion(f32[288,1152]{1,0:T(8,128)S(1)} %get-tuple-element.11, f32[288,1152]{1,0:T(8,128)S(1)} %get-tuple-element.10), kind=kLoop, calls=%fused_computation | loop fusion | flops 663552 | bytes 5308416 | tf_op jit(solution)/shard_map/transpose | solution.py:658

commit v3 on v2

--- a/solution.py
+++ b/solution.py
@@ -41,18 +41,18 @@
 
 class Sends:
     def __init__(self, sems):
-        self.sems, self.used, self.pending = sems, 0, []
-
-    def start(self, src, dst, recv_sem, where, cond=None):
+        self.sems, self.spots, self.pending = sems, {}, []
+
+    def start(self, src, dst, recv_sem, where, cond=None, spot=None):
+        spot = self.spots.setdefault(len(self.pending) if spot is None else spot, len(self.spots))
         copy = pltpu.make_async_remote_copy(
             src_ref=src,
             dst_ref=dst,
-            send_sem=self.sems.at[self.used],
+            send_sem=self.sems.at[spot],
             recv_sem=recv_sem,
             device_id=where,
             device_id_type=MESH,
         )
-        self.used += 1
         self.pending.append((cond, copy))
         guarded(cond, copy.start)
 
@@ -133,8 +133,8 @@
     def own_features(s, to_right, to_left, halves=range(2)):
         for h in halves:
             src = streams[s].at[pl.ds(h * half, half), :]
-            sends.start(src, feat_slot(s, h, col), feat_sem(s, h, col), right, to_right)
-            sends.start(src, feat_slot(s, h, col), feat_sem(s, h, col), left, to_left)
+            sends.start(src, feat_slot(s, h, col), feat_sem(s, h, col), right, to_right, ("own", s, h, 0))
+            sends.start(src, feat_slot(s, h, col), feat_sem(s, h, col), left, to_left, ("own", s, h, 1))
 
     def own_piece(p, wheres):
         w, r0, nr, _ = pieces[p]
@@ -167,10 +167,10 @@
             r_slot, r_sem = feat_slot(s, h, rb), feat_sem(s, h, rb)
             guarded(from_left, lambda: arrived(l_slot, l_sem))
             if step < n_col - 1:
-                sends.start(l_slot, l_slot, l_sem, right, from_left & has_right)
+                sends.start(l_slot, l_slot, l_sem, right, from_left & has_right, ("on", s, step, h, 0))
             guarded(from_right, lambda: arrived(r_slot, r_sem))
             if step < n_col - 1:
-                sends.start(r_slot, r_slot, r_sem, left, from_right & has_left)
+                sends.start(r_slot, r_slot, r_sem, left, from_right & has_left, ("on", s, step, h, 1))
 
     late_end = at_end if staggered else col < 0
     late_mid = middle if staggered else col < 0
@@ -282,9 +282,9 @@
     def term(w, rep):
         return jnp.dot(full[w // 2, rows_at(rep, 0, rows), :], grads[w], preferred_element_type=F32)
 
-    def pair_copy(i):
+    def pair_copy(i, spot=0):
         return pltpu.make_async_remote_copy(
-            src_ref=partner_out.at[lax.rem(i, 2 * peers)],
+            src_ref=partner_out.at[spot],
             dst_ref=sums.at[i],
             send_sem=pair_send.at[i],
             recv_sem=pair_recv.at[i],
@@ -297,7 +297,7 @@
     def stage_of(rep, late):
         block = (rep * rows) // feats
         dist = jnp.abs(block - col)
-        plain = jnp.maximum(dist - 1, 0)
+        plain = jnp.where(at_end, jnp.maximum(dist - 1, 0), 0)
         if not staggered:
             return plain
         second_half = lax.rem(rep, feats // rows) == 1
@@ -329,15 +329,16 @@
         late = pieces[p][0] // 2
         return second_in[late].at[k], second_sem[late].at[k]
 
-    def partner_term(w, dq, dy, when=None):
+    def partner_term(w, dq, dy, when=None, ahead=False):
         rep = rep_of(at_q(dq), 1 - c, at_y(dy))
         i = w * peers + at_q(dq) * ny + at_y(dy)
 
         def one():
-            if w == 0:
+            spot = 2 * peers if ahead else lax.rem(i, 2 * peers)
+            if w == 0 and not ahead:
                 pair_copy(2 * peers + i).wait_send()
-            partner_out[lax.rem(i, 2 * peers)] = term(w, rep).astype(BF16)
-            pair_copy(i).start()
+            partner_out[spot] = term(w, rep).astype(BF16)
+            pair_copy(i, spot).start()
 
         guarded(None if when is None else when(rep), one)
 
@@ -405,9 +406,11 @@
 
             guarded(cond, one)
             dst, sem = second_slot(p, d)
-            sends.start(sums.at[index, rs, :], dst, sem, y_peer(d) if route == 0 else q_peer(d), cond)
+            where = y_peer(d) if route == 0 else q_peer(d)
+            sends.start(sums.at[index, rs, :], dst, sem, where, cond, ("sum", p, d))
 
     outs = (og_ref, ou_ref, od_ref)
+    scale = 1.0 / math.sqrt(toks * n_dp * n_row)
 
     def second_own(p):
         w, r0, nr, route = pieces[p]
@@ -417,7 +420,7 @@
             ref, sem = first_slot(p, f, 0) if route == 0 else first_slot(p, 0, f)
             arrived(ref, sem)
             total = total + ref[...].astype(F32)
-        outs[w][rs, :] = total
+        outs[w][rs, :] = total * scale
 
     def second_final(p):
         w, r0, nr, route = pieces[p]
@@ -425,7 +428,33 @@
         for d in range(1, ny if route == 0 else nq):
             ref, sem = second_slot(p, d)
             arrived(ref, sem)
-            outs[w][rs, :] = outs[w][rs, :] + ref[...].astype(F32)
+            outs[w][rs, :] = outs[w][rs, :] + ref[...].astype(F32) * scale
+
+    at_block = lambda when_low, when_high: jnp.where(low, when_low, when_high) * feats
+    if staggered:
+        spans = [
+            [(at_block(0, 3), feats), (at_block(2, 1), feats)],
+            [(at_block(3, 0), feats), (at_block(1, 2), half)],
+            [(at_block(1, 2) + half, half)],
+        ]
+    else:
+        spans = [[(at_block(0, n_col - 1), feats)], [], [(at_block(n_col - 1, 0), feats)]]
+        if n_col > 2:
+            spans[1].append((feats + 0 * col, (n_col - 2) * feats))
+
+    def hidden_grad_over(phase):
+        if not spans[phase]:
+            return
+
+        @pl.loop(0, m_tiles)
+        def _(m):
+            ms = pl.ds(pl.multiple_of(m * mt, mt), mt)
+            part = None if phase == 0 else acc[ms, :]
+            for start, size in spans[phase]:
+                ks = pl.ds(pl.multiple_of(start, 16), size)
+                more = lax.dot_general(full[1, ks, ms], weights[2, ks, :], token_dims, preferred_element_type=F32)
+                part = more if part is None else part + more
+            acc[ms, :] = part
 
     stage_is = lambda k: lambda rep: own_stage(rep) == k
     on_time = jnp.logical_not(late_end)
@@ -440,53 +469,31 @@
             if staggered:
                 end_wait(k + 2, range(2), late_end)
         partner_terms(2, stage_is(k))
+        if k == last_stage - 1 and k > 0:
+            for p in later:
+                second_send(p, lambda k: k < last_stage - 1)
+            hidden_grad_over(1)
         own_terms(2, stage_is(k))
         if k == 0:
             for p in later:
                 near_rest(p)
             for p in later:
                 far(p)
-    for p in later:
-        from_partner(p)
-
-    inner = max(n_col - 2, 0) * feats
-    single = pl.multiple_of(jnp.where(low, 0, n_col - 1) * feats, 32)
-    pair = pl.multiple_of(jnp.where(late_end, jnp.where(low, 2, 0), 1) * feats, 32)
-    last = pl.multiple_of(
-        jnp.where(late_end, jnp.where(low, 1, n_col - 2), jnp.where(low, n_col - 1, 0)) * feats, 32)
-
-    @pl.loop(0, m_tiles)
-    def _(m):
-        ms = pl.ds(pl.multiple_of(m * mt, mt), mt)
-        ks = pl.ds(single, feats)
-        part = lax.dot_general(full[1, ks, ms], weights[2, ks, :], token_dims, preferred_element_type=F32)
-        if inner:
-            ks = pl.ds(pair, inner)
-            part = part + lax.dot_general(full[1, ks, ms], weights[2, ks, :], token_dims, preferred_element_type=F32)
-        acc[ms, :] = part
-
-    for p in later:
-        second_send(p, lambda k: k < last_stage - 1)
+            for p in later:
+                from_partner(p)
+            hidden_grad_over(0)
+
     end_wait(n_col - 1, range(2), on_time)
     if staggered:
         end_wait(1, [1], late_end)
-    partner_terms(2, stage_is(last_stage))
-
-    @pl.loop(0, m_tiles)
-    def _(m):
-        ms = pl.ds(pl.multiple_of(m * mt, mt), mt)
-        ks = pl.ds(last, feats)
-        acc[ms, :] = acc[ms, :] + lax.dot_general(
-            full[1, ks, ms], weights[2, ks, :], token_dims, preferred_element_type=F32)
-
+    hidden_grad_over(2)
     et = tile_of(toks, 32)
 
-    @pl.loop(0, toks // et)
-    def _(m):
-        ms = pl.ds(pl.multiple_of(m * et, et), et)
-        hidden_grad = acc[ms, :]
-        grads[0, ms, :] = (hidden_grad * stash[0, ms, :]).astype(BF16)
-        grads[1, ms, :] = (hidden_grad * stash[1, ms, :]).astype(BF16)
+    def finish_grad(w):
+        @pl.loop(0, toks // et)
+        def _(m):
+            ms = pl.ds(pl.multiple_of(m * et, et), et)
+            grads[w, ms, :] = (acc[ms, :] * stash[w, ms, :]).astype(BF16)
 
     rt = tile_of(feats, 288)
     hid_dims = (((1,), (1,)), ((), ()))
@@ -509,9 +516,9 @@
             for h in range(2):
                 src = lambda b: ig_out.at[b, pl.ds(h * half, half), :]
                 dst, sem = ig_slot(0, n_col - 1 - k, h)
-                sends.start(src(n_col - 1 - k), dst, sem, right, col == 0)
+                sends.start(src(n_col - 1 - k), dst, sem, right, col == 0, ("part", k, h))
                 dst, sem = ig_slot(1, k, h)
-                sends.start(src(k), dst, sem, left, col == n_col - 1)
+                sends.start(src(k), dst, sem, left, col == n_col - 1, ("part", k, h))
 
     def relay(going_left, k, side=None):
         d = k if going_left else n_col - 1 - k
@@ -527,18 +534,22 @@
                 part[...] = (part[...].astype(F32) + ref[...].astype(F32)).astype(BF16)
 
             guarded(inside, one)
-            sends.start(part, ref, sem, left if going_left else right, inside)
+            where = left if going_left else right
+            sends.start(part, ref, sem, where, inside, ("relay", going_left, k, h))
 
     sent = [[g for g in grid_order if g[0]], [g for g in grid_order if g[1]]]
     for i in range(max(len(sent[0]), len(sent[1]))):
         both = [(w, sent[w][i]) for w in range(2) if i < len(sent[w])]
         for w, place_i in both:
-            partner_term(w, *place_i)
+            if i == 0:
+                finish_grad(w)
+            partner_term(w, *place_i, ahead=w == 0 and i == 0)
         if i == 0:
-            own_terms(2, stage_is(last_stage))
+            partner_terms(2, stage_is(last_stage))
         for w, place_i in both:
             own_term(w, *place_i)
         if i == 0:
+            own_terms(2, stage_is(last_stage))
             for p in later:
                 second_send(p, lambda k: k == last_stage - 1)
             input_part(0)
@@ -599,6 +610,9 @@
         second_final(p)
     sends.finish()
 
+    dq, dy = sent[0][0]
+    pair_copy(2 * peers + at_q(dq) * ny + at_y(dy)).wait_send()
+
     @pl.loop(0, 2 * peers)
     def _(i):
         pair_copy(i).wait_send()
@@ -608,6 +622,21 @@
         def _(i):
             dq, dy = i // ny, i % ny
             pl.when((dq if route == 0 else dy) > 0)(slice_copy(p, dq, dy).wait_send)
+
+
+def flush(parts, *refs):
+    sems = refs[8]
+    copies = []
+    for i in range(4):
+        src, dst = refs[i], refs[4 + i]
+        pieces = next(n for n in range(parts, 0, -1) if n == 1 or src.shape[0] % (16 * n) == 0)
+        step = src.shape[0] // pieces
+        for j in range(pieces):
+            at = pl.ds(j * step, step)
+            copies.append(pltpu.make_async_copy(src.at[at, :], dst.at[at, :], sems.at[i * parts + j]))
+            copies[-1].start()
+    for copy in copies:
+        copy.wait()
 
 
 def body(n_dp, n_row, n_col, act_in, cot_out, w_gate, w_up, w_down):
@@ -622,8 +651,12 @@
         firsts[w // 2] += (nq - 1) * ny if route == 0 else (ny - 1) * nq
         seconds[w // 2] += (ny - 1) if route == 0 else (nq - 1)
     n_pieces = len(pieces)
-    n_sends = 24 + 8 * n_col + n_pieces * (nq + ny - 1) + n_pieces * (peers - 1) * max(nq, ny)
-    n_sends += sum(firsts) * 2 + sum(seconds) * 4 + 4 * (n_col - 1) + 8 * n_col * 3
+    n_sends = 8 + 8 * (n_col - 2)
+    n_sends += n_pieces * (nq + ny - 1)
+    for _, _, _, route in pieces:
+        n_sends += (nq - 1) * ny + ny - 1 if route == 0 else (ny - 1) * nq + nq - 1
+        n_sends += (nq - 1) * (ny - 1)
+    n_sends += sum(seconds) + 6 * (n_col - 1)
     late_rows = min(nr for w, _, nr, _ in pieces if w == 2)
     any_spec = pl.BlockSpec(memory_space=pl.ANY)
     dma = lambda n: pltpu.SemaphoreType.DMA((max(n, 1),))
@@ -640,7 +673,7 @@
             pltpu.VMEM((3, toks, hid), BF16),
             pltpu.VMEM((2, toks, hid), F32),
             pltpu.VMEM((toks, hid), F32),
-            pltpu.VMEM((2 * peers, rows, hid), BF16),
+            pltpu.VMEM((2 * peers + 1, rows, hid), BF16),
             pltpu.VMEM((3 * peers, rows, hid), BF16),
             landing(firsts),
             landing(seconds),
@@ -651,11 +684,19 @@
             dma(n_pieces * peers),
         ],
         compiler_params=pltpu.CompilerParams(
-            collective_id=0, has_side_effects=True, vmem_limit_bytes=60600000
+            collective_id=0, has_side_effects=True, vmem_limit_bytes=61400000
         ),
     )(act_in.T, cot_out.T, w_gate, w_up, w_down.T)
-    norm_scale = 1.0 / math.sqrt(toks * n_dp * n_row)
-    return (ig_t.T, gate_grad * norm_scale, up_grad * norm_scale, (down_t * norm_scale).T)
+    parts = 4
+    ig_t, gate_grad, up_grad, down_t = pl.pallas_call(
+        functools.partial(flush, parts),
+        out_shape=[jax.ShapeDtypeStruct((feats, toks), BF16)] + [jax.ShapeDtypeStruct((rows, hid), F32)] * 3,
+        in_specs=[pl.BlockSpec(memory_space=pltpu.VMEM)] * 4,
+        out_specs=[any_spec] * 4,
+        scratch_shapes=[dma(4 * parts)],
+        compiler_params=pltpu.CompilerParams(vmem_limit_bytes=1 << 20),
+    )(ig_t, gate_grad, up_grad, down_t)
+    return (ig_t.T, gate_grad, up_grad, down_t.T)
 
 
 def solution(mesh):

time: 146 us -> 143 us (0.979)
  other arithmetic: 2.82 us -> 0 us
    pallas_call x0 -> x1, Pallas kernels: none -> 2.27 us  [body(): pl.pallas_call(functools.partial(flush, parts), out_shape=[jax.ShapeDtype...]
    transpose x1 -> x0, other arithmetic: 1.67 us -> none  [body(): return (ig_t.T, gate_grad * norm_scale, up_grad * norm_scale, (down_t * n...]
    pallas_call x1, Pallas kernels: 142 us -> 140 us  [body(): pl.pallas_call(functools.partial(kernel, sizes), out_shape=[pltpu.VMEM((f...]
where the time goes in v3:
time: 143 us
  Pallas kernels  142 us (99%)
    pallas_call x1, Pallas kernels, body(): pl.pallas_call(functools.partial(kernel, sizes), out_shape=[pltpu.VMEM((f...  140 us

profile of v3, /device:TPU:5, one launch (start us, length us, event | category | flops | bytes accessed | tf_op | source)
XLA Modules:
  0.0 143.0 jit_solution(14070901505527431383)
XLA Ops:
  0.6 139.9 %shard_map.84 = (bf16[576,512]{1,0:T(8,128)(2,1)S(1)}, f32[288,1152]{1,0:T(8,128)S(1)}, f32[288,1152]{1,0:T(8,128)S(1)}, f32[288,1152]{1,0:T(8,128)S(1)}) custom-call(bf16[576,512]{1,0:T(8,128)(2,1)} %bitcast.6, bf16[576,512]{1,0:T(8,128)(2,1)} %bitcast.7, bf16[288,1152]{1,0:T(8,128)(2,1)} %wg_ref.1, bf16[288,1152]{1,0:T(8,128)(2,1)} %wu_ref.1, ...), custom_call_target="tpu_custom_call" | custom-call | tf_op jit(solution)/shard_map/pallas_call | solution.py:665
  140.6 2.3 %shard_map.85 = (bf16[576,512]{1,0:T(8,128)(2,1)}, f32[288,1152]{1,0:T(8,128)}, f32[288,1152]{1,0:T(8,128)}, f32[288,1152]{1,0:T(8,128)}) custom-call(bf16[576,512]{1,0:T(8,128)(2,1)S(1)} %get-tuple-element.12.refs_0_, f32[288,1152]{1,0:T(8,128)S(1)} %get-tuple-element.13.refs_1_, f32[288,1152]{1,0:T(8,128)S(1)} %get-tuple-element.14.refs_2_, ...), custom_call_target="tpu_custom_call" | custom-call | tf_op jit(solution)/shard_map/pallas_call | solution.py:691
